TPU v7x, 256 devices: a whole 4x4x8 slice. The times are simulated.
256 devices in a mesh: rows: 64 (over x, z_hi, y, core), feat: 4 (over z_lo).
Axes of the slice: x: 4, y: 4, z: 8 (z_hi: 2, z_lo: 4; z = z_hi * 4 + z_lo), core: 2. Of those that a mesh axis runs over, the one named last changes fastest.
Arguments:
- bins: int32 [65536, 512], P('rows', 'feat'), may hold values from -2147483648 to 2147483647, as said below
- hessian: float32 [262144], P('rows'), may hold values from 0.05 to 1
- thresholds: float32 [128], replicated, may hold values from 0.02 to 0.98
Outputs:
- cuts: float32 [512, 128], P('feat')
Inputs may be any that keep to these rules, and one draw needn't show every extreme that they name: `bins`: each word holds the bin ids, 0 to 255, of rows 4i to 4i + 3 of one feature, row 4i + k in bits 8k to 8k + 7 of the two's complement word.
All inputs are finite; a program needn't handle non-finite values.
Results may differ from a plain program's by a relative error of at most 0.000065.
Values sent between devices are 32-bit elements; how exact they have to be, the bound alone decides.
No kernel may reach another device: no remote copies, remote signals or barrier semaphores. Data moves between devices by JAX's collectives and lax.ppermute only.
A program may use at most 192 MiB of HBM per device.

v0:
```python
import math

import jax
import jax.numpy as jnp
from jax import lax
from jax.sharding import PartitionSpec as P

BINS = 256


def split_up(x, dim, devices):
    before, after = (x.shape[:dim], x.shape[dim + 1 :])
    return jnp.moveaxis(x.reshape(*before, devices, -1, *after), dim, 0)


def sent_and_summed(x, axis, dim):
    devices = lax.axis_size(axis)
    pieces = lax.all_to_all(split_up(x, dim, devices), axis, 0, 0, tiled=True)
    return jnp.sum(pieces, axis=0)


def joined_along(pieces, dim):
    pieces = jnp.moveaxis(pieces, 0, dim)
    lengths = pieces.shape
    return pieces.reshape(*lengths[:dim], lengths[dim] * lengths[dim + 1], *lengths[dim + 2 :])


def from_everyone(x, axis):
    copies = jnp.broadcast_to(x, (lax.axis_size(axis), *x.shape))
    return lax.all_to_all(copies, axis, split_axis=0, concat_axis=0, tiled=True)


def gather_directly(x, axis, dim):
    return joined_along(from_everyone(x, axis), dim)


def unpack(words):
    parts = [jnp.bitwise_and(jnp.right_shift(words, 8 * k), 255) for k in range(4)]
    stacked = jnp.stack(parts, axis=1)
    return stacked.reshape(words.shape[0] * 4, words.shape[1])


def histogram(columns, weights):
    count, width = columns.shape
    limit = max(8, 1048576 // (width * 16))
    block = math.gcd(count, limit)
    col_blocks = columns.reshape(count // block, block, width)
    wt_blocks = weights.reshape(count // block, block)
    levels = jnp.arange(16, dtype=jnp.int32)

    def add_block(total, item):
        col_part, wt_part = item
        high = jnp.right_shift(col_part, 4)
        low = jnp.bitwise_and(col_part, 15)
        high_hot = jnp.where(high[:, :, None] == levels, wt_part[:, None, None], 0.0)
        low_hot = (low[:, :, None] == levels).astype(jnp.float32)
        joint = jnp.einsum("rkh,rkl->khl", high_hot, low_hot, precision=lax.Precision.HIGHEST)
        return (total + joint, None)

    start = jnp.zeros((width, 16, 16), jnp.float32)
    total, unused = lax.scan(add_block, start, (col_blocks, wt_blocks))
    return total.reshape(width, BINS)


def cut_positions(hist, thresholds):
    cum = jnp.cumsum(hist, axis=1)
    before = cum - hist
    total = cum[:, -1]
    target = thresholds[None, :, None] * total[:, None, None]
    ratio = (target - before[:, None, :]) / (hist[:, None, :] + 1.0)
    return jnp.sum(jnp.clip(ratio, 0.0, 1.0), axis=2)


def local(bins, hessian, thresholds):
    local_ids = unpack(bins)
    hist = sent_and_summed(histogram(local_ids, hessian), "rows", 0)
    cuts = cut_positions(hist, thresholds)
    return gather_directly(cuts, "rows", 0)


def solution(mesh):
    in_specs = (P("rows", "feat"), P("rows"), P())
    out_specs = P("feat", None)
    return jax.shard_map(local, mesh=mesh, in_specs=in_specs, out_specs=out_specs, check_vma=False)
```

profile of v0, /device:TPU:1, one launch (start us, length us, event | category | flops | bytes accessed | tf_op | source)
XLA Modules:
  0.0 95.3 jit_solution(14017348286414728610)
XLA Ops:
  0.0 1.2 %and_bitcast_fusion.4 = (s32[1024,1,128]{2,0,1:T(8,128)S(1)}, s32[1024,1,128]{2,0,1:T(8,128)S(1)}, s32[1024,1,128]{2,0,1:T(8,128)S(1)}, s32[1024,1,128]{2,0,1:T(8,128)S(1)}) fusion(s32[1024,128]{1,0:T(8,128)} %param.5), kind=kLoop, calls=%fused_computation.19 | loop fusion | flops 1048576 | bytes 2621440 | tf_op jit(solution)/shard_map/stack | solution.py:39
  1.2 0.1 pad_add_fusion
  1.3 1.4 %copy.8 = s32[1024,4,128]{2,1,0:T(4,128)S(1)} copy(s32[1024,4,128]{2,0,1:T(8,128)S(1)} %pad_add_fusion) | data formatting | bytes 4194304 | tf_op jit(solution)/shard_map/stack | solution.py:39
  2.7 43.9 %while.12 = (s32[]{:T(128)}, f32[128,16,16]{2,1,0:T(8,128)}, s32[8,512,128]{2,1,0:T(8,128)S(1)}, f32[8,512]{1,0:T(8,128)S(1)}, s32[]{:T(128)}, /*index=5*/s32[]{:T(128)}) while((s32[]{:T(128)}, f32[128,16,16]{2,1,0:T(8,128)}, s32[8,512,128]{2,1,0:T(8,128)S(1)}, f32[8,512]{1,0:T(8,128)S(1)}, s32[]{:T(128)}, ...), condition=%wide.region_1.2_spmd.clone.clone, body=%wide.region_0.1_spmd.clone.clone.sunk | while | flops 204668928 | bytes 2627671 | solution.py:61
  2.8 0.1 copy.19
  3.0 4.2 %fusion.16 = f32[128,16,16]{2,1,0:T(8,128)} fusion(s32[512,128]{0,1:T(8,128)S(1)} %get-tuple-element.118, f32[512]{0:T(512)S(1)} %bitcast.30, s32[512,128]{0,1:T(8,128)S(1)} %get-tuple-element.119, f32[128,16,16]{2,1,0:T(8,128)} %get-tuple-element.127, pred[]{:T(512)S(6)} %compare.3), kind=kOutput, calls=%fused_computation.9.clone.1 | convolution fusion | flops 204537856 | bytes 788481 | tf_op jit(solution)/shard_map/while/body/eval_jaxpr/rkh,rkl->khl/dot_general | solution.py:57
  7.2 0.1 copy.19
  7.4 5.4 %fusion.16 = f32[128,16,16]{2,1,0:T(8,128)} fusion(s32[512,128]{0,1:T(8,128)S(1)} %get-tuple-element.118, f32[512]{0:T(512)S(1)} %bitcast.30, s32[512,128]{0,1:T(8,128)S(1)} %get-tuple-element.119, f32[128,16,16]{2,1,0:T(8,128)} %get-tuple-element.127, pred[]{:T(512)S(6)} %compare.3), kind=kOutput, calls=%fused_computation.9.clone.1 | convolution fusion | flops 204537856 | bytes 788481 | tf_op jit(solution)/shard_map/while/body/eval_jaxpr/rkh,rkl->khl/dot_general | solution.py:57
  12.8 0.1 copy.19
  13.1 5.4 %fusion.16 = f32[128,16,16]{2,1,0:T(8,128)} fusion(s32[512,128]{0,1:T(8,128)S(1)} %get-tuple-element.118, f32[512]{0:T(512)S(1)} %bitcast.30, s32[512,128]{0,1:T(8,128)S(1)} %get-tuple-element.119, f32[128,16,16]{2,1,0:T(8,128)} %get-tuple-element.127, pred[]{:T(512)S(6)} %compare.3), kind=kOutput, calls=%fused_computation.9.clone.1 | convolution fusion | flops 204537856 | bytes 788481 | tf_op jit(solution)/shard_map/while/body/eval_jaxpr/rkh,rkl->khl/dot_general | solution.py:57
  18.7 5.4 %fusion.16 = f32[128,16,16]{2,1,0:T(8,128)} fusion(s32[512,128]{0,1:T(8,128)S(1)} %get-tuple-element.118, f32[512]{0:T(512)S(1)} %bitcast.30, s32[512,128]{0,1:T(8,128)S(1)} %get-tuple-element.119, f32[128,16,16]{2,1,0:T(8,128)} %get-tuple-element.127, pred[]{:T(512)S(6)} %compare.3), kind=kOutput, calls=%fused_computation.9.clone.1 | convolution fusion | flops 204537856 | bytes 788481 | tf_op jit(solution)/shard_map/while/body/eval_jaxpr/rkh,rkl->khl/dot_general | solution.py:57
  24.4 5.4 %fusion.16 = f32[128,16,16]{2,1,0:T(8,128)} fusion(s32[512,128]{0,1:T(8,128)S(1)} %get-tuple-element.118, f32[512]{0:T(512)S(1)} %bitcast.30, s32[512,128]{0,1:T(8,128)S(1)} %get-tuple-element.119, f32[128,16,16]{2,1,0:T(8,128)} %get-tuple-element.127, pred[]{:T(512)S(6)} %compare.3), kind=kOutput, calls=%fused_computation.9.clone.1 | convolution fusion | flops 204537856 | bytes 788481 | tf_op jit(solution)/shard_map/while/body/eval_jaxpr/rkh,rkl->khl/dot_general | solution.py:57
  30.0 5.4 %fusion.16 = f32[128,16,16]{2,1,0:T(8,128)} fusion(s32[512,128]{0,1:T(8,128)S(1)} %get-tuple-element.118, f32[512]{0:T(512)S(1)} %bitcast.30, s32[512,128]{0,1:T(8,128)S(1)} %get-tuple-element.119, f32[128,16,16]{2,1,0:T(8,128)} %get-tuple-element.127, pred[]{:T(512)S(6)} %compare.3), kind=kOutput, calls=%fused_computation.9.clone.1 | convolution fusion | flops 204537856 | bytes 788481 | tf_op jit(solution)/shard_map/while/body/eval_jaxpr/rkh,rkl->khl/dot_general | solution.py:57
  35.4 0.1 copy.19
  35.6 5.4 %fusion.16 = f32[128,16,16]{2,1,0:T(8,128)} fusion(s32[512,128]{0,1:T(8,128)S(1)} %get-tuple-element.118, f32[512]{0:T(512)S(1)} %bitcast.30, s32[512,128]{0,1:T(8,128)S(1)} %get-tuple-element.119, f32[128,16,16]{2,1,0:T(8,128)} %get-tuple-element.127, pred[]{:T(512)S(6)} %compare.3), kind=kOutput, calls=%fused_computation.9.clone.1 | convolution fusion | flops 204537856 | bytes 788481 | tf_op jit(solution)/shard_map/while/body/eval_jaxpr/rkh,rkl->khl/dot_general | solution.py:57
  41.3 5.4 %fusion.16 = f32[128,16,16]{2,1,0:T(8,128)} fusion(s32[512,128]{0,1:T(8,128)S(1)} %get-tuple-element.118, f32[512]{0:T(512)S(1)} %bitcast.30, s32[512,128]{0,1:T(8,128)S(1)} %get-tuple-element.119, f32[128,16,16]{2,1,0:T(8,128)} %get-tuple-element.127, pred[]{:T(512)S(6)} %compare.3), kind=kOutput, calls=%fused_computation.9.clone.1 | convolution fusion | flops 204537856 | bytes 788481 | tf_op jit(solution)/shard_map/while/body/eval_jaxpr/rkh,rkl->khl/dot_general | solution.py:57
  46.7 1.7 %reshape_reshape.7 = f32[64,2,256]{2,1,0:T(2,128)S(1)} reshape(f32[128,16,16]{2,1,0:T(8,128)} %get-tuple-element.35) | data formatting | bytes 262144 | tf_op jit(solution)/shard_map/reshape;reshape | solution.py:13
  48.4 27.9 %all_to_all.10 = f32[64,2,256]{2,1,0:T(2,128)S(1)} all-to-all(f32[64,2,256]{2,1,0:T(2,128)S(1)} %reshape_reshape.7), channel_id=1, replica_groups=mesh['rows'=64,'feat'=4] {'rows'}, dimensions={0} | all-to-all | bytes 262144 | tf_op jit(solution)/shard_map/all_to_all | solution.py:18
  76.4 0.6 reduce-window.6
  77.0 0.2 slice_reduce_fusion
  77.2 0.2 reduce-window.9
  77.7 0.2 clamp_reduce_fusion
  77.9 16.8 %all_to_all.11 = f32[64,2,128]{2,1,0:T(2,128)S(1)} all-to-all(f32[64,2,128]{2,1,0:T(2,128)S(1)} %broadcast_in_dim.29), channel_id=1, replica_groups=mesh['rows'=64,'feat'=4] {'rows'}, dimensions={0} | all-to-all | bytes 131072 | tf_op jit(solution)/shard_map/all_to_all | solution.py:30
  94.7 0.6 copy.27
  (43 shorter events, 1.7 us)
Async XLA Ops:
  1.3 1.4 %copy-start = (f32[4096]{0:T(1024)S(1)}, f32[4096]{0:T(1024)}, u32[]{:S(2)}) copy-start(f32[4096]{0:T(1024)} %param.6) | copy-start | bytes 49156
  2.7 74.9 %copy-start.1 = (f32[128]{0:T(128)S(1)}, f32[128]{0:T(128)}, u32[]{:S(2)}) copy-start(f32[128]{0:T(128)} %param.7) | copy-start | bytes 1540
where the time goes:
time: 95.8 us; the launch traced here: 95.3 us
  blocking collectives  44.7 us (47%)
  matrix products  42 us (44%)
  local copies, waits for them, and re-layouts  5.36 us (6%)
  other arithmetic  2.98 us (3%)
    dot_general x8, matrix products, add_block(): jnp.einsum('rkh,rkl->khl', high_hot, low_hot, precision=lax.Precision.HIG...  42 us
    all_to_all x1, blocking collectives, sent_and_summed(): pieces = lax.all_to_all(split_up(x, dim, devices), axis, 0, 0, tiled=True)  27.9 us
    all_to_all x1, blocking collectives, from_everyone(): return lax.all_to_all(copies, axis, split_axis=0, concat_axis=0, tiled=True)  16.8 us

commit v1 on v0

v1 whole, which is shorter than its diff:
```python
import jax
import jax.numpy as jnp
from jax import lax
from jax.experimental import pallas as pl
from jax.experimental.pallas import tpu as pltpu
from jax.sharding import Mesh
from jax.sharding import PartitionSpec as P

BINS = 256
HI = 8
LO = 32
GROUP = 8
TERMS = 2


def hist_kernel(bins_ref, hess_ref, out_ref, words_ref, wts_ref):
    words, width = bins_ref.shape
    for i in range(words // 128):
        words_ref[:, pl.ds(128 * i, 128)] = bins_ref[pl.ds(128 * i, 128), :].T
    rest = hess_ref[...]
    for t in range(TERMS):
        part = rest.astype(jnp.bfloat16)
        rest = rest - part.astype(jnp.float32)
        for k in range(4):
            wts_ref[t, k] = jnp.broadcast_to(part[k : k + 1, :], (16, words))
    own = lax.broadcasted_iota(jnp.int32, (HI, GROUP, LO * GROUP), 2) % GROUP == lax.broadcasted_iota(
        jnp.int32, (HI, GROUP, LO * GROUP), 1
    )

    def pairs(x):
        return jnp.concatenate([x, x - 1], axis=0).astype(jnp.float32).astype(jnp.bfloat16)

    def group(g, carry):
        word = words_ref[pl.ds(pl.multiple_of(g * GROUP, GROUP), GROUP), :]
        total = jnp.zeros((TERMS * HI * GROUP, LO * GROUP), jnp.float32)
        for k in range(4):
            for c in range(words // 256):
                part = word[:, 256 * c : 256 * (c + 1)]
                high = pairs(jnp.bitwise_and(jnp.right_shift(part, 8 * k + 5), 7))
                low = pairs(jnp.bitwise_and(jnp.right_shift(part, 8 * k), 31))
                left = []
                for t in range(TERMS):
                    w = wts_ref[t, k, :, 256 * c : 256 * (c + 1)]
                    left += [jnp.where(high == 2 * p, w, jnp.bfloat16(0)) for p in range(HI // 2)]
                right = [
                    jnp.where(low == 2 * p, jnp.bfloat16(1), jnp.bfloat16(0)) for p in range(LO // 2)
                ]
                total += lax.dot_general(
                    jnp.concatenate(left, axis=0),
                    jnp.concatenate(right, axis=0),
                    (((1,), (1,)), ((), ())),
                    preferred_element_type=jnp.float32,
                )
        joint = jnp.sum(total.reshape(TERMS, HI, GROUP, LO * GROUP), axis=0)
        out_ref[g] = jnp.sum(jnp.where(own, joint, 0.0), axis=1)
        return carry

    lax.fori_loop(0, width // GROUP, group, 0)


def histogram(bins, hessian):
    words, width = bins.shape
    weights = hessian.reshape(words, 4).T
    return pl.pallas_call(
        hist_kernel,
        out_shape=jax.ShapeDtypeStruct((width // GROUP, HI, LO * GROUP), jnp.float32),
        scratch_shapes=[
            pltpu.VMEM((width, words), jnp.int32),
            pltpu.VMEM((TERMS, 4, 16, words), jnp.bfloat16),
        ],
        name="histogram",
    )(bins, weights)


def cuts_kernel(a_ref, b_ref, thr_ref, out_ref):
    lanes = LO * GROUP
    n_q = thr_ref.shape[1]
    hist = a_ref[...] + b_ref[...]
    src = lax.broadcasted_iota(jnp.int32, (lanes, lanes), 0)
    dst = lax.broadcasted_iota(jnp.int32, (lanes, lanes), 1)
    same = src % GROUP == dst % GROUP
    earlier = jnp.where(same & (src < dst), 1.0, 0.0)
    row = jnp.where(same, 1.0, 0.0)
    dot = lambda x, y: jnp.dot(x, y, precision=lax.Precision.HIGHEST, preferred_element_type=jnp.float32)
    before = dot(hist, earlier)
    sums = dot(hist, row)
    offset = jnp.zeros((1, lanes), jnp.float32)
    offsets = []
    for i in range(HI):
        offsets.append(offset)
        offset = offset + sums[i : i + 1, :]
    before = before + jnp.concatenate(offsets, axis=0)
    scale = 1.0 / (hist + 1.0)
    thr = jnp.broadcast_to(thr_ref[...], (n_q, n_q)).T
    halves = []
    for j in range(lanes // n_q):
        at = slice(n_q * j, n_q * (j + 1))
        target = thr * offset[:, at]
        acc = jnp.zeros((n_q, n_q), jnp.float32)
        for i in range(HI):
            acc += jnp.clip((target - before[i : i + 1, at]) * scale[i : i + 1, at], 0.0, 1.0)
        halves.append(acc)
    acc = halves[0] + halves[1]
    pick = jnp.where(
        lax.broadcasted_iota(jnp.int32, (GROUP, n_q), 1) % GROUP
        == lax.broadcasted_iota(jnp.int32, (GROUP, n_q), 0),
        1.0,
        0.0,
    )
    cuts = lax.dot_general(
        pick,
        acc,
        (((1,), (1,)), ((), ())),
        precision=lax.Precision.HIGHEST,
        preferred_element_type=jnp.float32,
    )
    out_ref[...] = jnp.broadcast_to(cuts[None], out_ref.shape)


def cut_positions(a, b, thresholds, copies):
    n_q = thresholds.shape[0]
    return pl.pallas_call(
        cuts_kernel,
        out_shape=jax.ShapeDtypeStruct((copies, GROUP, n_q), jnp.float32),
        name="cuts",
    )(a, b, thresholds.reshape(1, n_q))


def local(bins, hessian, thresholds):
    swap = [(0, 1), (1, 0)]
    pieces = histogram(bins, hessian)
    pieces = lax.all_to_all(pieces, ("x", "y"), 0, 0, tiled=True)
    part = jnp.sum(pieces, axis=0)
    part = part + lax.ppermute(part, "core", swap)
    other = lax.ppermute(part, "far", swap)
    copies = cut_positions(part, other, thresholds, pieces.shape[0])
    cuts = lax.all_to_all(copies, ("x", "y"), 0, 0, tiled=True)
    return cuts.reshape(bins.shape[1], thresholds.shape[0])


def solution(mesh):
    feat = mesh.shape["feat"]
    axes = ("x", "far", "y", "core")
    grid = Mesh(mesh.devices.reshape(4, 2, 4, 2, feat), axes + ("feat",))
    in_specs = (P(axes, "feat"), P(axes), P())
    out_specs = P("feat", None)
    return jax.shard_map(local, mesh=grid, in_specs=in_specs, out_specs=out_specs, check_vma=False)
```

time: 95.8 us -> 56.6 us (0.59)
  matrix products: 42 us -> 0 us
  blocking collectives: 44.7 us -> 24.4 us
  Pallas kernels: 0 us -> 17.6 us
  starting transfers between devices: 0 us -> 8.93 us
  other arithmetic: 2.98 us -> 0.02 us
  local copies, waits for them, and re-layouts: 5.36 us -> 3.27 us
  waiting for transfers between devices: 0 us -> 1.87 us
    dot_general x8 -> x0, matrix products: 42 us -> none  [add_block(): jnp.einsum('rkh,rkl->khl', high_hot, low_hot, precision=lax.Precision.HIG...]
    all_to_all x2, blocking collectives: 44.7 us -> 24.4 us  [the longest x1 14.4 us: local(): pieces = lax.all_to_all(pieces, ('x', 'y'), 0, 0, tiled=True)]
    pallas_call x0 -> x2, Pallas kernels: none -> 17.6 us  [the longest x1 15.4 us: histogram(): pl.pallas_call(hist_kernel, out_shape=jax.ShapeDtypeStruct((width // GROU...]
    ppermute x0 -> x2, starting transfers between devices: none -> 8.93 us  [the longest x1 6.91 us: local(): other = lax.ppermute(part, 'far', swap)]
    another operation x2 -> x0, local copies, waits for them, and re-layouts: 3.08 us -> none  [the longest x1 1.73 us: split_up(): return jnp.moveaxis(x.reshape(*before, devices, -1, *after), dim, 0)]
    another operation x4 -> x0, other arithmetic: 2.1 us -> none  [the longest x2 1.32 us: unpack(): stacked = jnp.stack(parts, axis=1)]
    reshape x2, local copies, waits for them, and re-layouts: 0.02 us -> 2.04 us  [histogram(): weights = hessian.reshape(words, 4).T]
    ppermute x0 -> x2, waiting for transfers between devices: none -> 1.87 us  [the longest x1 1.04 us: local(): other = lax.ppermute(part, 'far', swap)]
  transfers between devices with their start and end apart: 0 -> 2, of which waited for: 0 -> 2; matrix products, arithmetic and copies ran while one was open for 0% -> 0% of each run, Pallas kernels for 0% -> 0%
where the time goes in v1:
time: 56.6 us; the launch traced here: 56.1 us
  blocking collectives  24.4 us (43%)
  Pallas kernels  17.6 us (31%)
  starting transfers between devices  8.93 us (16%)
  local copies, waits for them, and re-layouts  3.27 us (6%)
  waiting for transfers between devices  1.87 us (3%)
    pallas_call x1, Pallas kernels, histogram(): pl.pallas_call(hist_kernel, out_shape=jax.ShapeDtypeStruct((width // GROU...  15.4 us
    all_to_all x1, blocking collectives, local(): pieces = lax.all_to_all(pieces, ('x', 'y'), 0, 0, tiled=True)  14.4 us
    all_to_all x1, blocking collectives, local(): cuts = lax.all_to_all(copies, ('x', 'y'), 0, 0, tiled=True)  9.94 us
    ppermute x1, starting transfers between devices, local(): other = lax.ppermute(part, 'far', swap)  6.91 us
    pallas_call x1, Pallas kernels, cut_positions(): pl.pallas_call(cuts_kernel, out_shape=jax.ShapeDtypeStruct((copies, GROUP...  2.22 us
    reshape x2, local copies, waits for them, and re-layouts, histogram(): weights = hessian.reshape(words, 4).T  2.04 us
    ppermute x1, starting transfers between devices, local(): part = part + lax.ppermute(part, 'core', swap)  2.02 us
    unnamed x5, local copies, waits for them, and re-layouts  1.23 us
  transfers between devices with their start and end apart: 2, of which 2 were waited for; matrix products, arithmetic and copies ran while one was open for 0% of the time, Pallas kernels for 0%

profile of v1, /device:TPU:1, one launch (start us, length us, event | category | flops | bytes accessed | tf_op | source)
XLA Modules:
  0.0 56.1 jit_solution(15982124543743395881)
XLA Ops:
  0.0 1.2 %reshape.9 = f32[1024,4]{1,0:T(8,128)S(1)} reshape(f32[4096]{0:T(1024)} %param.4) | data formatting | bytes 32768 | tf_op jit(solution)/shard_map/reshape | solution.py:63
  1.3 0.8 %copy.4 = f32[1024,4]{0,1:T(4,128)} copy(f32[1024,4]{1,0:T(8,128)S(1)} %reshape.9) | data formatting | bytes 32768 | tf_op jit(solution)/shard_map/reshape | solution.py:63
  2.0 15.4 %histogram.1 = f32[16,8,256]{2,1,0:T(8,128)} custom-call(s32[1024,128]{1,0:T(8,128)} %bins_ref.1, f32[4,1024]{1,0:T(4,128)} %bitcast.4), custom_call_target="tpu_custom_call" | custom-call | tf_op jit(solution)/shard_map/histogram/pallas_call | solution.py:64
  17.4 14.4 %all_to_all.10 = f32[16,8,256]{2,1,0:T(8,128)S(1)} all-to-all(f32[16,8,256]{2,1,0:T(8,128)} %histogram.1), channel_id=1, replica_groups=mesh['x'=4,'far'=2,'y'=4,'core'=2,'feat'=4] {'x','y'}, dimensions={0} | all-to-all | bytes 262144 | tf_op jit(solution)/shard_map/all_to_all | solution.py:132
  31.9 2.0 %collective-permute-start = (f32[8,256]{1,0:T(8,128)S(1)}, f32[8,256]{1,0:T(8,128)S(1)}, u32[]{:S(2)}, u32[]{:S(2)}) collective-permute-start(f32[8,256]{1,0:T(8,128)S(1)} %reduce_sum.9), channel_id=1, source_target_pairs={{0,4},{4,0},{1,5},{5,1},{2,6},{6,2},{3,7},{7,3},{8,12},{12,8},{9,1... | collective-permute-start | bytes 24584 | tf_op jit(solution)/shard_map/ppermute | solution.py:134
  33.9 0.8 %collective-permute-done = f32[8,256]{1,0:T(8,128)S(1)} collective-permute-done((f32[8,256]{1,0:T(8,128)S(1)}, f32[8,256]{1,0:T(8,128)S(1)}, u32[]{:S(2)}, u32[]{:S(2)}) %collective-permute-start) | collective-permute-done | bytes 8224 | tf_op jit(solution)/shard_map/ppermute | solution.py:134
  34.8 0.0 copy-start
  34.8 6.9 %collective-permute-start.1 = (f32[8,256]{1,0:T(8,128)S(1)}, f32[8,256]{1,0:T(8,128)S(1)}, u32[]{:S(2)}, u32[]{:S(2)}) collective-permute-start(f32[8,256]{1,0:T(8,128)S(1)} %add.3.a_ref), channel_id=1, source_target_pairs={{0,32},{32,0},{1,33},{33,1},{2,34},{34,2},{3,35},{35,3},{4,36},{36... | collective-permute-start | bytes 24584 | tf_op jit(solution)/shard_map/ppermute | solution.py:135
  41.7 1.0 %collective-permute-done.1.b_ref = f32[8,256]{1,0:T(8,128)S(1)} collective-permute-done((f32[8,256]{1,0:T(8,128)S(1)}, f32[8,256]{1,0:T(8,128)S(1)}, u32[]{:S(2)}, u32[]{:S(2)}) %collective-permute-start.1) | collective-permute-done | bytes 8224 | tf_op jit(solution)/shard_map/ppermute | solution.py:135
  42.7 0.0 copy-start.1
  42.7 0.0 copy-done
  42.7 0.6 %copy-done.1 = f32[8,256]{1,0:T(8,128)} copy-done((f32[8,256]{1,0:T(8,128)}, f32[8,256]{1,0:T(8,128)S(1)}, u32[]{:S(2)}) %copy-start.1) | copy-done | bytes 8216
  43.3 2.2 %cuts.1 = f32[16,8,128]{2,1,0:T(8,128)} custom-call(f32[8,256]{1,0:T(8,128)} %copy-done, f32[8,256]{1,0:T(8,128)} %copy-done.1, f32[1,128]{1,0:T(1,128)} %bitcast.5), custom_call_target="tpu_custom_call" | custom-call | tf_op jit(solution)/shard_map/cuts/pallas_call | solution.py:122
  45.5 9.9 %all_to_all.11 = f32[16,8,128]{2,1,0:T(8,128)S(1)} all-to-all(f32[16,8,128]{2,1,0:T(8,128)} %cuts.1), channel_id=1, replica_groups=mesh['x'=4,'far'=2,'y'=4,'core'=2,'feat'=4] {'x','y'}, dimensions={0} | all-to-all | bytes 131072 | tf_op jit(solution)/shard_map/all_to_all | solution.py:137
  55.5 0.6 %copy.6 = f32[128,128]{1,0:T(8,128)} copy(f32[128,128]{1,0:T(8,128)S(1)} %bitcast.3) | data formatting | bytes 131072
  (2 shorter events, 0.0 us)
Async XLA Ops:
  31.9 2.8 %collective-permute-start = (f32[8,256]{1,0:T(8,128)S(1)}, f32[8,256]{1,0:T(8,128)S(1)}, u32[]{:S(2)}, u32[]{:S(2)}) collective-permute-start(f32[8,256]{1,0:T(8,128)S(1)} %reduce_sum.9), channel_id=1, source_target_pairs={{0,4},{4,0},{1,5},{5,1},{2,6},{6,2},{3,7},{7,3},{8,12},{12,8},{9,1... | collective-permute-start | bytes 24584 | tf_op jit(solution)/shard_map/ppermute | solution.py:134
  34.8 8.0 %copy-start = (f32[8,256]{1,0:T(8,128)}, f32[8,256]{1,0:T(8,128)S(1)}, u32[]{:S(2)}) copy-start(f32[8,256]{1,0:T(8,128)S(1)} %add.3.a_ref) | copy-start | bytes 24580
  34.8 8.0 %collective-permute-start.1 = (f32[8,256]{1,0:T(8,128)S(1)}, f32[8,256]{1,0:T(8,128)S(1)}, u32[]{:S(2)}, u32[]{:S(2)}) collective-permute-start(f32[8,256]{1,0:T(8,128)S(1)} %add.3.a_ref), channel_id=1, source_target_pairs={{0,32},{32,0},{1,33},{33,1},{2,34},{34,2},{3,35},{35,3},{4,36},{36... | collective-permute-start | bytes 24584 | tf_op jit(solution)/shard_map/ppermute | solution.py:135
  42.7 0.6 %copy-start.1 = (f32[8,256]{1,0:T(8,128)}, f32[8,256]{1,0:T(8,128)S(1)}, u32[]{:S(2)}) copy-start(f32[8,256]{1,0:T(8,128)S(1)} %collective-permute-done.1.b_ref) | copy-start | bytes 24580

commit v2 on v1

v2 whole, which is shorter than its diff:
```python
import jax
import jax.numpy as jnp
from jax import lax
from jax.experimental import pallas as pl
from jax.experimental.pallas import tpu as pltpu
from jax.sharding import Mesh
from jax.sharding import PartitionSpec as P

BINS = 256
HI = 8
LO = 32
GROUP = 8
PIECE = 4
TERMS = 2
LANES = 128
UNROLL = 16


def iota(shape, dim):
    return lax.broadcasted_iota(jnp.int32, shape, dim)


def hist_kernel(
    bins_hbm, hess_hbm, thr_hbm, out_ref, thr_ref, bins_ref, hess_ref, words_ref, wide_ref, wts_ref, sems
):
    words, width = bins_ref.shape
    blocks = words // LANES
    hess_copy = pltpu.make_async_copy(hess_hbm, hess_ref, sems.at[blocks])
    hess_copy.start()
    copies = []
    for i in range(blocks):
        at = pl.ds(LANES * i, LANES)
        copies.append(pltpu.make_async_copy(bins_hbm.at[at, :], bins_ref.at[at, :], sems.at[i]))
        copies[-1].start()
    thr_copy = pltpu.make_async_copy(thr_hbm, thr_ref, sems.at[blocks + 1])
    thr_copy.start()

    hess_copy.wait()
    lane = iota((blocks, LANES), 1)
    rows = [hess_ref[pl.ds(j, blocks, stride=4), :] for j in range(4)]
    for k in range(4):
        index = 4 * (lane % 32) + k
        weight = jnp.zeros((blocks, LANES), jnp.float32)
        for j in range(4):
            weight = jnp.where(lane // 32 == j, jnp.take_along_axis(rows[j], index, axis=1), weight)
        for t in range(TERMS):
            part = weight.astype(jnp.bfloat16).astype(jnp.float32)
            weight = weight - part
            for i in range(blocks):
                wts_ref[t, k, :, LANES * i : LANES * (i + 1)] = jnp.broadcast_to(
                    part[i : i + 1, :], (16, LANES)
                ).astype(jnp.bfloat16)

    for i in range(blocks):
        copies[i].wait()
        at = slice(LANES * i, LANES * (i + 1))
        turned = bins_ref[at, :].T
        words_ref[:, at] = turned
        for p in range(width // PIECE):
            four = turned[PIECE * p : PIECE * (p + 1), :]
            wide_ref[2 * PIECE * p : 2 * PIECE * (p + 1), at] = jnp.concatenate([four, four], axis=0)

    own = iota((HI, GROUP, LANES), 2) % PIECE == iota((HI, GROUP, LANES), 1) % PIECE
    first = iota((HI, GROUP, LANES), 1) < PIECE
    step16 = iota((16, LANES), 0)
    one = jnp.bfloat16(1)
    zero = jnp.bfloat16(0)

    def halves(x):
        x = jnp.concatenate([x, x], axis=0)
        return x.astype(jnp.int16), jnp.right_shift(x, 16).astype(jnp.int16)

    def group(g, carry):
        total = jnp.zeros((TERMS * HI * GROUP, 2 * LANES), jnp.float32)
        for c in range(words // 256):
            at = slice(256 * c, 256 * (c + 1))
            high = halves(words_ref[pl.ds(pl.multiple_of(g * GROUP, GROUP), GROUP), at])
            low = [
                halves(wide_ref[pl.ds(pl.multiple_of((2 * g + s) * GROUP, GROUP), GROUP), at]) for s in range(2)
            ]
            for k in range(4):
                shift = 8 * (k % 2)
                top = jnp.bitwise_and(high[k // 2], jnp.int16(int_of(224 << shift)))
                ends = [jnp.bitwise_and(low[s][k // 2], jnp.int16(31 << shift)) for s in range(2)]
                left = []
                hits = [
                    top == jnp.tile(shifted(2 * p + step16 // 8, shift + 5), (1, 2)) for p in range(HI // 2)
                ]
                for t in range(TERMS):
                    w = wts_ref[t, k, :, at]
                    left += [jnp.where(hit, w, zero) for hit in hits]
                right = [
                    jnp.where(ends[s] == jnp.tile(shifted(4 * p + step16 // 4, shift), (1, 2)), one, zero)
                    for s in range(2)
                    for p in range(LO // 4)
                ]
                total += lax.dot_general(
                    jnp.concatenate(left, axis=0),
                    jnp.concatenate(right, axis=0).astype(jnp.float8_e4m3fn),
                    (((1,), (1,)), ((), ())),
                    preferred_element_type=jnp.float32,
                )
        joint = jnp.sum(total.reshape(TERMS, HI, GROUP, 2 * LANES), axis=0)
        for s in range(2):
            keep = own & (first if s == 0 else ~first)
            out_ref[2 * g + s] = jnp.sum(jnp.where(keep, joint[:, :, LANES * s : LANES * (s + 1)], 0.0), axis=1)
        return carry

    lax.fori_loop(0, width // GROUP, group, 0, unroll=UNROLL)
    thr_copy.wait()


def int_of(x):
    return x - 65536 if x >= 32768 else x


def shifted(x, by):
    return jnp.left_shift(x, by).astype(jnp.int16)


def histogram(bins, hessian, thresholds):
    words, width = bins.shape
    n_q = thresholds.shape[0]
    hbm = pl.BlockSpec(memory_space=pl.ANY)
    return pl.pallas_call(
        hist_kernel,
        out_shape=(
            pltpu.VMEM((width // PIECE, HI, LO * PIECE), jnp.float32),
            pltpu.VMEM((1, n_q), jnp.float32),
        ),
        in_specs=[hbm, hbm, hbm],
        out_specs=(pl.BlockSpec(memory_space=pltpu.VMEM),) * 2,
        scratch_shapes=[
            pltpu.VMEM((words, width), jnp.int32),
            pltpu.VMEM((hessian.shape[0] // LANES, LANES), jnp.float32),
            pltpu.VMEM((width, words), jnp.int32),
            pltpu.VMEM((2 * width, words), jnp.int32),
            pltpu.VMEM((TERMS, 4, 16, words), jnp.bfloat16),
            pltpu.SemaphoreType.DMA((words // LANES + 2,)),
        ],
        name="histogram",
    )(bins, hessian.reshape(-1, LANES), thresholds.reshape(1, n_q))


def terms_of(x):
    parts = []
    for _ in range(2):
        parts.append(x.astype(jnp.bfloat16).astype(jnp.float32))
        x = x - parts[-1]
    return parts + [x]


def cuts_kernel(a_ref, b_ref, thr_ref, out_ref):
    hist = a_ref[...] + b_ref[...]
    src = iota((LANES, LANES), 0)
    dst = iota((LANES, LANES), 1)
    same = src % PIECE == dst % PIECE
    ones = jnp.concatenate([jnp.where(same & (src < dst), 1.0, 0.0), jnp.where(same, 1.0, 0.0)], axis=1)
    sums = jnp.dot(
        jnp.concatenate(terms_of(hist), axis=0).astype(jnp.bfloat16),
        ones.astype(jnp.bfloat16),
        preferred_element_type=jnp.float32,
    )
    sums = sums[:HI] + sums[HI : 2 * HI] + sums[2 * HI :]
    offset = jnp.zeros((1, LANES), jnp.float32)
    offsets = []
    for i in range(HI):
        offsets.append(offset)
        offset = offset + sums[i : i + 1, LANES:]
    before = sums[:, :LANES] + jnp.concatenate(offsets, axis=0)
    scale = 1.0 / (hist + 1.0)
    target = jnp.broadcast_to(thr_ref[...], (LANES, LANES)).T * offset
    acc = jnp.zeros(target.shape, jnp.float32)
    for i in range(HI):
        acc += jnp.clip((target - before[i : i + 1]) * scale[i : i + 1], 0.0, 1.0)
    n_q = acc.shape[0]
    pick = jnp.where(iota((16, LANES), 1) % PIECE == iota((16, LANES), 0), 1.0, 0.0)
    cuts = lax.dot_general(
        pick.astype(jnp.bfloat16),
        jnp.concatenate(terms_of(acc), axis=0).astype(jnp.bfloat16),
        (((1,), (1,)), ((), ())),
        preferred_element_type=jnp.float32,
    )
    cuts = cuts[:PIECE, :n_q] + cuts[:PIECE, n_q : 2 * n_q] + cuts[:PIECE, 2 * n_q :]
    out_ref[...] = jnp.broadcast_to(cuts[None], out_ref.shape)


def cut_positions(a, b, thr, copies):
    return pl.pallas_call(
        cuts_kernel,
        out_shape=pltpu.VMEM((copies, PIECE, thr.shape[1]), jnp.float32),
        in_specs=[pl.BlockSpec(memory_space=pltpu.VMEM)] * 3,
        out_specs=pl.BlockSpec(memory_space=pltpu.VMEM),
        name="cuts",
    )(*(pltpu.with_memory_space_constraint(x, pltpu.VMEM) for x in (a, b, thr)))


def local(bins, hessian, thresholds):
    near = ("x", "y", "core")
    pieces, thr = histogram(bins, hessian, thresholds)
    pieces = lax.all_to_all(pieces, near, 0, 0, tiled=True)
    part = jnp.sum(pieces, axis=0)
    other = lax.ppermute(part, "far", [(0, 1), (1, 0)])
    copies = cut_positions(part, other, thr, pieces.shape[0])
    cuts = lax.all_to_all(copies, near, 0, 0, tiled=True)
    return cuts.reshape(bins.shape[1], thresholds.shape[0])


def solution(mesh):
    feat = mesh.shape["feat"]
    axes = ("x", "far", "y", "core")
    grid = Mesh(mesh.devices.reshape(4, 2, 4, 2, feat), axes + ("feat",))
    in_specs = (P(axes, "feat"), P(axes), P())
    out_specs = P("feat", None)
    return jax.shard_map(local, mesh=grid, in_specs=in_specs, out_specs=out_specs, check_vma=False)
```

time: 56.6 us -> 43.4 us (0.77)
  Pallas kernels: 17.6 us -> 6.64 us
  blocking collectives: 24.4 us -> 27.9 us
  local copies, waits for them, and re-layouts: 3.27 us -> 0.63 us
  starting transfers between devices: 8.93 us -> 6.99 us
  waiting for transfers between devices: 1.87 us -> 1 us
    pallas_call x2, Pallas kernels: 17.6 us -> 6.64 us  [the longest x1 6.28 us: histogram(): pl.pallas_call(hist_kernel, out_shape=(pltpu.VMEM((width // PIECE, HI, LO...]
    all_to_all x2, blocking collectives: 24.4 us -> 27.9 us  [the longest x1 16.1 us: local(): pieces = lax.all_to_all(pieces, near, 0, 0, tiled=True)]
    reshape x2 -> x0, local copies, waits for them, and re-layouts: 2.04 us -> none  [histogram(): weights = hessian.reshape(words, 4).T]
    ppermute x2 -> x1, starting transfers between devices: 8.93 us -> 6.99 us  [local(): other = lax.ppermute(part, 'far', [(0, 1), (1, 0)])]
    ppermute x2 -> x1, waiting for transfers between devices: 1.87 us -> 1 us  [local(): other = lax.ppermute(part, 'far', [(0, 1), (1, 0)])]
    unnamed x5 -> x1, local copies, waits for them, and re-layouts: 1.23 us -> 0.63 us
  transfers between devices with their start and end apart: 2 -> 1, of which waited for: 2 -> 1; matrix products, arithmetic and copies ran while one was open for 0% -> 0% of each run, Pallas kernels for 0% -> 0%
where the time goes in v2:
time: 43.4 us; the launch traced here: 43.2 us
  blocking collectives  27.9 us (64%)
  starting transfers between devices  6.99 us (16%)
  Pallas kernels  6.64 us (15%)
  waiting for transfers between devices  1 us (2%)
  local copies, waits for them, and re-layouts  0.63 us (1%)
    all_to_all x1, blocking collectives, local(): pieces = lax.all_to_all(pieces, near, 0, 0, tiled=True)  16.1 us
    all_to_all x1, blocking collectives, local(): cuts = lax.all_to_all(copies, near, 0, 0, tiled=True)  11.8 us
    ppermute x1, starting transfers between devices, local(): other = lax.ppermute(part, 'far', [(0, 1), (1, 0)])  6.99 us
    pallas_call x1, Pallas kernels, histogram(): pl.pallas_call(hist_kernel, out_shape=(pltpu.VMEM((width // PIECE, HI, LO...  6.28 us
    ppermute x1, waiting for transfers between devices, local(): other = lax.ppermute(part, 'far', [(0, 1), (1, 0)])  1 us
  transfers between devices with their start and end apart: 1, of which 1 were waited for; matrix products, arithmetic and copies ran while one was open for 0% of the time, Pallas kernels for 0%

profile of v2, /device:TPU:1, one launch (start us, length us, event | category | flops | bytes accessed | tf_op | source)
XLA Modules:
  0.0 43.2 jit_solution(15744060183889763242)
XLA Ops:
  0.0 6.3 %histogram.1 = (f32[32,8,128]{2,1,0:T(8,128)S(1)}, f32[1,128]{1,0:T(1,128)S(1)}) custom-call(s32[1024,128]{1,0:T(8,128)} %bins_hbm.1, f32[32,128]{1,0:T(8,128)} %bitcast.4, f32[1,128]{1,0:T(1,128)} %bitcast.5), custom_call_target="tpu_custom_call" | custom-call | tf_op jit(solution)/shard_map/histogram/pallas_call | solution.py:125
  6.3 16.1 %all_to_all.10 = f32[32,8,128]{2,1,0:T(8,128)S(1)} all-to-all(f32[32,8,128]{2,1,0:T(8,128)S(1)} %get-tuple-element.7), channel_id=1, replica_groups=mesh['x'=4,'far'=2,'y'=4,'core'=2,'feat'=4] {'x','y','core'}, dimensions={0} | all-to-all | bytes 262144 | tf_op jit(solution)/shard_map/all_to_all | solution.py:201
  22.4 7.0 %collective-permute-start = (f32[8,128]{1,0:T(8,128)S(1)}, f32[8,128]{1,0:T(8,128)S(1)}, u32[]{:S(2)}, u32[]{:S(2)}) collective-permute-start(f32[8,128]{1,0:T(8,128)S(1)} %reduce_sum.9.a_ref), channel_id=1, source_target_pairs={{0,32},{32,0},{1,33},{33,1},{2,34},{34,2},{3,35},{35,3},{4,36},{36... | collective-permute-start | bytes 12296 | tf_op jit(solution)/shard_map/ppermute | solution.py:203
  29.4 1.0 %collective-permute-done.b_ref = f32[8,128]{1,0:T(8,128)S(1)} collective-permute-done((f32[8,128]{1,0:T(8,128)S(1)}, f32[8,128]{1,0:T(8,128)S(1)}, u32[]{:S(2)}, u32[]{:S(2)}) %collective-permute-start) | collective-permute-done | bytes 4128 | tf_op jit(solution)/shard_map/ppermute | solution.py:203
  30.4 0.4 cuts.1
  30.7 11.8 %all_to_all.11 = f32[32,4,128]{2,1,0:T(4,128)S(1)} all-to-all(f32[32,4,128]{2,1,0:T(4,128)S(1)} %cuts.1), channel_id=1, replica_groups=mesh['x'=4,'far'=2,'y'=4,'core'=2,'feat'=4] {'x','y','core'}, dimensions={0} | all-to-all | bytes 131072 | tf_op jit(solution)/shard_map/all_to_all | solution.py:205
  42.5 0.6 %copy.5 = f32[128,128]{1,0:T(8,128)} copy(f32[128,128]{1,0:T(8,128)S(1)} %bitcast.3) | data formatting | bytes 131072
  (1 shorter events, 0.0 us)
Async XLA Ops:
  22.4 8.0 %collective-permute-start = (f32[8,128]{1,0:T(8,128)S(1)}, f32[8,128]{1,0:T(8,128)S(1)}, u32[]{:S(2)}, u32[]{:S(2)}) collective-permute-start(f32[8,128]{1,0:T(8,128)S(1)} %reduce_sum.9.a_ref), channel_id=1, source_target_pairs={{0,32},{32,0},{1,33},{33,1},{2,34},{34,2},{3,35},{35,3},{4,36},{36... | collective-permute-start | bytes 12296 | tf_op jit(solution)/shard_map/ppermute | solution.py:203

commit v3 on v2

--- a/solution.py
+++ b/solution.py
@@ -25,17 +25,24 @@
 ):
     words, width = bins_ref.shape
     blocks = words // LANES
-    hess_copy = pltpu.make_async_copy(hess_hbm, hess_ref, sems.at[blocks])
-    hess_copy.start()
-    copies = []
+    copies = [
+        pltpu.make_async_copy(hess_hbm, hess_ref, sems.at[0]),
+        pltpu.make_async_copy(bins_hbm, bins_ref, sems.at[1]),
+        pltpu.make_async_copy(thr_hbm, thr_ref, sems.at[2]),
+    ]
+    for copy in copies:
+        copy.start()
+    for copy in copies:
+        copy.wait()
+
     for i in range(blocks):
-        at = pl.ds(LANES * i, LANES)
-        copies.append(pltpu.make_async_copy(bins_hbm.at[at, :], bins_ref.at[at, :], sems.at[i]))
-        copies[-1].start()
-    thr_copy = pltpu.make_async_copy(thr_hbm, thr_ref, sems.at[blocks + 1])
-    thr_copy.start()
-
-    hess_copy.wait()
+        at = slice(LANES * i, LANES * (i + 1))
+        turned = bins_ref[at, :].T
+        words_ref[:, at] = turned
+        for p in range(width // PIECE):
+            four = turned[PIECE * p : PIECE * (p + 1), :]
+            wide_ref[2 * PIECE * p : 2 * PIECE * (p + 1), at] = jnp.concatenate([four, four], axis=0)
+
     lane = iota((blocks, LANES), 1)
     rows = [hess_ref[pl.ds(j, blocks, stride=4), :] for j in range(4)]
     for k in range(4):
@@ -50,15 +57,6 @@
                 wts_ref[t, k, :, LANES * i : LANES * (i + 1)] = jnp.broadcast_to(
                     part[i : i + 1, :], (16, LANES)
                 ).astype(jnp.bfloat16)
-
-    for i in range(blocks):
-        copies[i].wait()
-        at = slice(LANES * i, LANES * (i + 1))
-        turned = bins_ref[at, :].T
-        words_ref[:, at] = turned
-        for p in range(width // PIECE):
-            four = turned[PIECE * p : PIECE * (p + 1), :]
-            wide_ref[2 * PIECE * p : 2 * PIECE * (p + 1), at] = jnp.concatenate([four, four], axis=0)
 
     own = iota((HI, GROUP, LANES), 2) % PIECE == iota((HI, GROUP, LANES), 1) % PIECE
     first = iota((HI, GROUP, LANES), 1) < PIECE
@@ -107,7 +105,6 @@
         return carry
 
     lax.fori_loop(0, width // GROUP, group, 0, unroll=UNROLL)
-    thr_copy.wait()
 
 
 def int_of(x):
@@ -136,7 +133,7 @@
             pltpu.VMEM((width, words), jnp.int32),
             pltpu.VMEM((2 * width, words), jnp.int32),
             pltpu.VMEM((TERMS, 4, 16, words), jnp.bfloat16),
-            pltpu.SemaphoreType.DMA((words // LANES + 2,)),
+            pltpu.SemaphoreType.DMA((3,)),
         ],
         name="histogram",
     )(bins, hessian.reshape(-1, LANES), thresholds.reshape(1, n_q))

time: 43.4 us -> 43 us (level)
  no operation moved by 1% of the time
where the time goes in v3:
time: 43 us; the launch traced here: 42.8 us
  blocking collectives  27.9 us (65%)
  starting transfers between devices  6.98 us (16%)
  Pallas kernels  6.22 us (14%)
  waiting for transfers between devices  1 us (2%)
  local copies, waits for them, and re-layouts  0.63 us (1%)
    all_to_all x1, blocking collectives, local(): pieces = lax.all_to_all(pieces, near, 0, 0, tiled=True)  16.1 us
    all_to_all x1, blocking collectives, local(): cuts = lax.all_to_all(copies, near, 0, 0, tiled=True)  11.8 us
    ppermute x1, starting transfers between devices, local(): other = lax.ppermute(part, 'far', [(0, 1), (1, 0)])  6.98 us
    pallas_call x1, Pallas kernels, histogram(): pl.pallas_call(hist_kernel, out_shape=(pltpu.VMEM((width // PIECE, HI, LO...  5.86 us
    ppermute x1, waiting for transfers between devices, local(): other = lax.ppermute(part, 'far', [(0, 1), (1, 0)])  1 us
  transfers between devices with their start and end apart: 1, of which 1 were waited for; matrix products, arithmetic and copies ran while one was open for 0% of the time, Pallas kernels for 0%

profile of v3, /device:TPU:1, one launch (start us, length us, event | category | flops | bytes accessed | tf_op | source)
XLA Modules:
  0.0 42.8 jit_solution(2143300555067149385)
XLA Ops:
  0.0 5.9 %histogram.1 = (f32[32,8,128]{2,1,0:T(8,128)S(1)}, f32[1,128]{1,0:T(1,128)S(1)}) custom-call(s32[1024,128]{1,0:T(8,128)} %bins_hbm.1, f32[32,128]{1,0:T(8,128)} %bitcast.4, f32[1,128]{1,0:T(1,128)} %bitcast.5), custom_call_target="tpu_custom_call" | custom-call | tf_op jit(solution)/shard_map/histogram/pallas_call | solution.py:122
  5.9 16.1 %all_to_all.10 = f32[32,8,128]{2,1,0:T(8,128)S(1)} all-to-all(f32[32,8,128]{2,1,0:T(8,128)S(1)} %get-tuple-element.7), channel_id=1, replica_groups=mesh['x'=4,'far'=2,'y'=4,'core'=2,'feat'=4] {'x','y','core'}, dimensions={0} | all-to-all | bytes 262144 | tf_op jit(solution)/shard_map/all_to_all | solution.py:198
  22.0 7.0 %collective-permute-start = (f32[8,128]{1,0:T(8,128)S(1)}, f32[8,128]{1,0:T(8,128)S(1)}, u32[]{:S(2)}, u32[]{:S(2)}) collective-permute-start(f32[8,128]{1,0:T(8,128)S(1)} %reduce_sum.9.a_ref), channel_id=1, source_target_pairs={{0,32},{32,0},{1,33},{33,1},{2,34},{34,2},{3,35},{35,3},{4,36},{36... | collective-permute-start | bytes 12296 | tf_op jit(solution)/shard_map/ppermute | solution.py:200
  28.9 1.0 %collective-permute-done.b_ref = f32[8,128]{1,0:T(8,128)S(1)} collective-permute-done((f32[8,128]{1,0:T(8,128)S(1)}, f32[8,128]{1,0:T(8,128)S(1)}, u32[]{:S(2)}, u32[]{:S(2)}) %collective-permute-start) | collective-permute-done | bytes 4128 | tf_op jit(solution)/shard_map/ppermute | solution.py:200
  29.9 0.4 cuts.1
  30.3 11.8 %all_to_all.11 = f32[32,4,128]{2,1,0:T(4,128)S(1)} all-to-all(f32[32,4,128]{2,1,0:T(4,128)S(1)} %cuts.1), channel_id=1, replica_groups=mesh['x'=4,'far'=2,'y'=4,'core'=2,'feat'=4] {'x','y','core'}, dimensions={0} | all-to-all | bytes 131072 | tf_op jit(solution)/shard_map/all_to_all | solution.py:202
  42.1 0.6 %copy.5 = f32[128,128]{1,0:T(8,128)} copy(f32[128,128]{1,0:T(8,128)S(1)} %bitcast.3) | data formatting | bytes 131072
  (1 shorter events, 0.0 us)
Async XLA Ops:
  22.0 8.0 %collective-permute-start = (f32[8,128]{1,0:T(8,128)S(1)}, f32[8,128]{1,0:T(8,128)S(1)}, u32[]{:S(2)}, u32[]{:S(2)}) collective-permute-start(f32[8,128]{1,0:T(8,128)S(1)} %reduce_sum.9.a_ref), channel_id=1, source_target_pairs={{0,32},{32,0},{1,33},{33,1},{2,34},{34,2},{3,35},{35,3},{4,36},{36... | collective-permute-start | bytes 12296 | tf_op jit(solution)/shard_map/ppermute | solution.py:200

commit v4 on v3

--- a/solution.py
+++ b/solution.py
@@ -3,7 +3,6 @@
 from jax import lax
 from jax.experimental import pallas as pl
 from jax.experimental.pallas import tpu as pltpu
-from jax.sharding import Mesh
 from jax.sharding import PartitionSpec as P
 
 BINS = 256
@@ -192,21 +191,35 @@
     )(*(pltpu.with_memory_space_constraint(x, pltpu.VMEM) for x in (a, b, thr)))
 
 
+def groups_of(first):
+    x0, y0, c0 = first
+    return [
+        [
+            (((x0 + x) % 4 * 2 + far) * 4 + (y0 + y) % 4) * 2 + (c0 + c) % 2
+            for x in range(4)
+            for y in range(4)
+            for c in range(2)
+        ]
+        for far in range(2)
+    ]
+
+
+FIRST = (2, 2, 1)
+
+
 def local(bins, hessian, thresholds):
-    near = ("x", "y", "core")
+    near = groups_of(FIRST)
+    swap = [(i, i ^ 8) for i in range(64)]
     pieces, thr = histogram(bins, hessian, thresholds)
-    pieces = lax.all_to_all(pieces, near, 0, 0, tiled=True)
+    pieces = lax.all_to_all(pieces, "rows", 0, 0, axis_index_groups=near, tiled=True)
     part = jnp.sum(pieces, axis=0)
-    other = lax.ppermute(part, "far", [(0, 1), (1, 0)])
+    other = lax.ppermute(part, "rows", swap)
     copies = cut_positions(part, other, thr, pieces.shape[0])
-    cuts = lax.all_to_all(copies, near, 0, 0, tiled=True)
+    cuts = lax.all_to_all(copies, "rows", 0, 0, axis_index_groups=near, tiled=True)
     return cuts.reshape(bins.shape[1], thresholds.shape[0])
 
 
 def solution(mesh):
-    feat = mesh.shape["feat"]
-    axes = ("x", "far", "y", "core")
-    grid = Mesh(mesh.devices.reshape(4, 2, 4, 2, feat), axes + ("feat",))
-    in_specs = (P(axes, "feat"), P(axes), P())
+    in_specs = (P("rows", "feat"), P("rows"), P())
     out_specs = P("feat", None)
-    return jax.shard_map(local, mesh=grid, in_specs=in_specs, out_specs=out_specs, check_vma=False)
+    return jax.shard_map(local, mesh=mesh, in_specs=in_specs, out_specs=out_specs, check_vma=False)

time: 43 us -> 38.6 us (0.90)
  blocking collectives: 27.9 us -> 23.6 us
    all_to_all x2, blocking collectives: 27.9 us -> 23.6 us  [the longest x1 12.5 us: local(): lax.all_to_all(pieces, 'rows', 0, 0, axis_index_groups=near, tiled=True)]
where the time goes in v4:
time: 38.6 us; the launch traced here: 38.4 us
  blocking collectives  23.6 us (61%)
  starting transfers between devices  6.91 us (18%)
  Pallas kernels  6.22 us (16%)
  waiting for transfers between devices  1 us (3%)
  local copies, waits for them, and re-layouts  0.63 us (2%)
    all_to_all x1, blocking collectives, local(): lax.all_to_all(pieces, 'rows', 0, 0, axis_index_groups=near, tiled=True)  12.5 us
    all_to_all x1, blocking collectives, local(): lax.all_to_all(copies, 'rows', 0, 0, axis_index_groups=near, tiled=True)  11.1 us
    ppermute x1, starting transfers between devices, local(): other = lax.ppermute(part, 'rows', swap)  6.91 us
    pallas_call x1, Pallas kernels, histogram(): pl.pallas_call(hist_kernel, out_shape=(pltpu.VMEM((width // PIECE, HI, LO...  5.86 us
    ppermute x1, waiting for transfers between devices, local(): other = lax.ppermute(part, 'rows', swap)  1 us
  transfers between devices with their start and end apart: 1, of which 1 were waited for; matrix products, arithmetic and copies ran while one was open for 0% of the time, Pallas kernels for 0%

profile of v4, /device:TPU:1, one launch (start us, length us, event | category | flops | bytes accessed | tf_op | source)
XLA Modules:
  0.0 38.4 jit_solution(8559442531082951483)
XLA Ops:
  0.0 5.9 %histogram.1 = (f32[32,8,128]{2,1,0:T(8,128)S(1)}, f32[1,128]{1,0:T(1,128)S(1)}) custom-call(s32[1024,128]{1,0:T(8,128)} %bins_hbm.1, f32[32,128]{1,0:T(8,128)} %bitcast.4, f32[1,128]{1,0:T(1,128)} %bitcast.5), custom_call_target="tpu_custom_call" | custom-call | tf_op jit(solution)/shard_map/histogram/pallas_call | solution.py:121
  5.9 12.5 %all_to_all.10 = f32[32,8,128]{2,1,0:T(8,128)S(1)} all-to-all(f32[32,8,128]{2,1,0:T(8,128)S(1)} %get-tuple-element.7), channel_id=1, replica_groups={{148,144,156,152,132,128,140,136,212,208,220,216,196,192,204,200,20,16,..., dimensions={0} | all-to-all | bytes 262144 | tf_op jit(solution)/shard_map/all_to_all | solution.py:214
  18.4 6.9 %collective-permute-start = (f32[8,128]{1,0:T(8,128)S(1)}, f32[8,128]{1,0:T(8,128)S(1)}, u32[]{:S(2)}, u32[]{:S(2)}) collective-permute-start(f32[8,128]{1,0:T(8,128)S(1)} %reduce_sum.9.a_ref), channel_id=1, source_target_pairs={{0,32},{4,36},{8,40},{12,44},{16,48},{20,52},{24,56},{28,60},{32,0... | collective-permute-start | bytes 12296 | tf_op jit(solution)/shard_map/ppermute | solution.py:216
  25.3 1.0 %collective-permute-done.b_ref = f32[8,128]{1,0:T(8,128)S(1)} collective-permute-done((f32[8,128]{1,0:T(8,128)S(1)}, f32[8,128]{1,0:T(8,128)S(1)}, u32[]{:S(2)}, u32[]{:S(2)}) %collective-permute-start) | collective-permute-done | bytes 4128 | tf_op jit(solution)/shard_map/ppermute | solution.py:216
  26.3 0.4 cuts.1
  26.7 11.1 %all_to_all.11 = f32[32,4,128]{2,1,0:T(4,128)S(1)} all-to-all(f32[32,4,128]{2,1,0:T(4,128)S(1)} %cuts.1), channel_id=1, replica_groups={{148,144,156,152,132,128,140,136,212,208,220,216,196,192,204,200,20,16,..., dimensions={0} | all-to-all | bytes 131072 | tf_op jit(solution)/shard_map/all_to_all | solution.py:218
  37.8 0.6 %copy.5 = f32[128,128]{1,0:T(8,128)} copy(f32[128,128]{1,0:T(8,128)S(1)} %bitcast.3) | data formatting | bytes 131072
  (1 shorter events, 0.0 us)
Async XLA Ops:
  18.4 7.9 %collective-permute-start = (f32[8,128]{1,0:T(8,128)S(1)}, f32[8,128]{1,0:T(8,128)S(1)}, u32[]{:S(2)}, u32[]{:S(2)}) collective-permute-start(f32[8,128]{1,0:T(8,128)S(1)} %reduce_sum.9.a_ref), channel_id=1, source_target_pairs={{0,32},{4,36},{8,40},{12,44},{16,48},{20,52},{24,56},{28,60},{32,0... | collective-permute-start | bytes 12296 | tf_op jit(solution)/shard_map/ppermute | solution.py:216

commit v5 on v4

--- a/solution.py
+++ b/solution.py
@@ -195,7 +195,7 @@
     x0, y0, c0 = first
     return [
         [
-            (((x0 + x) % 4 * 2 + far) * 4 + (y0 + y) % 4) * 2 + (c0 + c) % 2
+            (((x0 + x) % 4 * 2 + far) * 4 + (y0 + y) % 4) * 2 + (c0 + c + 1 - far) % 2
             for x in range(4)
             for y in range(4)
             for c in range(2)
@@ -209,7 +209,7 @@
 
 def local(bins, hessian, thresholds):
     near = groups_of(FIRST)
-    swap = [(i, i ^ 8) for i in range(64)]
+    swap = [(i, i ^ 9) for i in range(64)]
     pieces, thr = histogram(bins, hessian, thresholds)
     pieces = lax.all_to_all(pieces, "rows", 0, 0, axis_index_groups=near, tiled=True)
     part = jnp.sum(pieces, axis=0)

time: 38.6 us -> 38.4 us (level)
  blocking collectives: 23.6 us -> 22.8 us
    all_to_all x1, blocking collectives: 11.1 us -> 10 us  [local(): lax.all_to_all(copies, 'rows', 0, 0, axis_index_groups=near, tiled=True)]
where the time goes in v5:
time: 38.4 us; the launch traced here: 38.1 us
  blocking collectives  22.8 us (59%)
  starting transfers between devices  7.09 us (18%)
  Pallas kernels  6.22 us (16%)
  waiting for transfers between devices  1.29 us (3%)
  local copies, waits for them, and re-layouts  0.63 us (2%)
    all_to_all x1, blocking collectives, local(): lax.all_to_all(pieces, 'rows', 0, 0, axis_index_groups=near, tiled=True)  12.8 us
    all_to_all x1, blocking collectives, local(): lax.all_to_all(copies, 'rows', 0, 0, axis_index_groups=near, tiled=True)  10 us
    ppermute x1, starting transfers between devices, local(): other = lax.ppermute(part, 'rows', swap)  7.09 us
    pallas_call x1, Pallas kernels, histogram(): pl.pallas_call(hist_kernel, out_shape=(pltpu.VMEM((width // PIECE, HI, LO...  5.86 us
    ppermute x1, waiting for transfers between devices, local(): other = lax.ppermute(part, 'rows', swap)  1.29 us
  transfers between devices with their start and end apart: 1, of which 1 were waited for; matrix products, arithmetic and copies ran while one was open for 0% of the time, Pallas kernels for 0%

profile of v5, /device:TPU:1, one launch (start us, length us, event | category | flops | bytes accessed | tf_op | source)
XLA Modules:
  0.0 38.1 jit_solution(14142839923672858162)
XLA Ops:
  0.0 5.9 %histogram.1 = (f32[32,8,128]{2,1,0:T(8,128)S(1)}, f32[1,128]{1,0:T(1,128)S(1)}) custom-call(s32[1024,128]{1,0:T(8,128)} %bins_hbm.1, f32[32,128]{1,0:T(8,128)} %bitcast.4, f32[1,128]{1,0:T(1,128)} %bitcast.5), custom_call_target="tpu_custom_call" | custom-call | tf_op jit(solution)/shard_map/histogram/pallas_call | solution.py:121
  5.9 12.8 %all_to_all.10 = f32[32,8,128]{2,1,0:T(8,128)S(1)} all-to-all(f32[32,8,128]{2,1,0:T(8,128)S(1)} %get-tuple-element.7), channel_id=1, replica_groups={{144,148,152,156,128,132,136,140,208,212,216,220,192,196,200,204,16,20,..., dimensions={0} | all-to-all | bytes 262144 | tf_op jit(solution)/shard_map/all_to_all | solution.py:214
  18.7 7.1 %collective-permute-start = (f32[8,128]{1,0:T(8,128)S(1)}, f32[8,128]{1,0:T(8,128)S(1)}, u32[]{:S(2)}, u32[]{:S(2)}) collective-permute-start(f32[8,128]{1,0:T(8,128)S(1)} %reduce_sum.9.a_ref), channel_id=1, source_target_pairs={{0,36},{4,32},{8,44},{12,40},{16,52},{20,48},{24,60},{28,56},{32,4... | collective-permute-start | bytes 12296 | tf_op jit(solution)/shard_map/ppermute | solution.py:216
  25.8 1.3 %collective-permute-done.b_ref = f32[8,128]{1,0:T(8,128)S(1)} collective-permute-done((f32[8,128]{1,0:T(8,128)S(1)}, f32[8,128]{1,0:T(8,128)S(1)}, u32[]{:S(2)}, u32[]{:S(2)}) %collective-permute-start) | collective-permute-done | bytes 4128 | tf_op jit(solution)/shard_map/ppermute | solution.py:216
  27.1 0.4 cuts.1
  27.5 10.0 %all_to_all.11 = f32[32,4,128]{2,1,0:T(4,128)S(1)} all-to-all(f32[32,4,128]{2,1,0:T(4,128)S(1)} %cuts.1), channel_id=1, replica_groups={{144,148,152,156,128,132,136,140,208,212,216,220,192,196,200,204,16,20,..., dimensions={0} | all-to-all | bytes 131072 | tf_op jit(solution)/shard_map/all_to_all | solution.py:218
  37.5 0.6 %copy.5 = f32[128,128]{1,0:T(8,128)} copy(f32[128,128]{1,0:T(8,128)S(1)} %bitcast.3) | data formatting | bytes 131072
  (1 shorter events, 0.0 us)
Async XLA Ops:
  18.7 8.4 %collective-permute-start = (f32[8,128]{1,0:T(8,128)S(1)}, f32[8,128]{1,0:T(8,128)S(1)}, u32[]{:S(2)}, u32[]{:S(2)}) collective-permute-start(f32[8,128]{1,0:T(8,128)S(1)} %reduce_sum.9.a_ref), channel_id=1, source_target_pairs={{0,36},{4,32},{8,44},{12,40},{16,52},{20,48},{24,60},{28,56},{32,4... | collective-permute-start | bytes 12296 | tf_op jit(solution)/shard_map/ppermute | solution.py:216

commit v6 on v5

--- a/solution.py
+++ b/solution.py
@@ -25,13 +25,13 @@
     words, width = bins_ref.shape
     blocks = words // LANES
     copies = [
-        pltpu.make_async_copy(hess_hbm, hess_ref, sems.at[0]),
-        pltpu.make_async_copy(bins_hbm, bins_ref, sems.at[1]),
+        pltpu.make_async_copy(bins_hbm, bins_ref, sems.at[0]),
+        pltpu.make_async_copy(hess_hbm, hess_ref, sems.at[1]),
         pltpu.make_async_copy(thr_hbm, thr_ref, sems.at[2]),
     ]
     for copy in copies:
         copy.start()
-    for copy in copies:
+    for copy in copies[:2]:
         copy.wait()
 
     for i in range(blocks):
@@ -104,6 +104,7 @@
         return carry
 
     lax.fori_loop(0, width // GROUP, group, 0, unroll=UNROLL)
+    copies[2].wait()
 
 
 def int_of(x):

time: 38.4 us -> 38.3 us (level)
  no operation moved by 1% of the time
where the time goes in v6:
time: 38.3 us; the launch traced here: 38.1 us
  blocking collectives  22.8 us (60%)
  starting transfers between devices  7.09 us (19%)
  Pallas kernels  6.21 us (16%)
  waiting for transfers between devices  1.29 us (3%)
  local copies, waits for them, and re-layouts  0.63 us (2%)
    all_to_all x1, blocking collectives, local(): lax.all_to_all(pieces, 'rows', 0, 0, axis_index_groups=near, tiled=True)  12.8 us
    all_to_all x1, blocking collectives, local(): lax.all_to_all(copies, 'rows', 0, 0, axis_index_groups=near, tiled=True)  10 us
    ppermute x1, starting transfers between devices, local(): other = lax.ppermute(part, 'rows', swap)  7.09 us
    pallas_call x1, Pallas kernels, histogram(): pl.pallas_call(hist_kernel, out_shape=(pltpu.VMEM((width // PIECE, HI, LO...  5.85 us
    ppermute x1, waiting for transfers between devices, local(): other = lax.ppermute(part, 'rows', swap)  1.29 us
  transfers between devices with their start and end apart: 1, of which 1 were waited for; matrix products, arithmetic and copies ran while one was open for 0% of the time, Pallas kernels for 0%

profile of v6, /device:TPU:1, one launch (start us, length us, event | category | flops | bytes accessed | tf_op | source)
XLA Modules:
  0.0 38.1 jit_solution(15160697187106766084)
XLA Ops:
  0.0 5.8 %histogram.1 = (f32[32,8,128]{2,1,0:T(8,128)S(1)}, f32[1,128]{1,0:T(1,128)S(1)}) custom-call(s32[1024,128]{1,0:T(8,128)} %bins_hbm.1, f32[32,128]{1,0:T(8,128)} %bitcast.4, f32[1,128]{1,0:T(1,128)} %bitcast.5), custom_call_target="tpu_custom_call" | custom-call | tf_op jit(solution)/shard_map/histogram/pallas_call | solution.py:122
  5.9 12.8 %all_to_all.10 = f32[32,8,128]{2,1,0:T(8,128)S(1)} all-to-all(f32[32,8,128]{2,1,0:T(8,128)S(1)} %get-tuple-element.7), channel_id=1, replica_groups={{144,148,152,156,128,132,136,140,208,212,216,220,192,196,200,204,16,20,..., dimensions={0} | all-to-all | bytes 262144 | tf_op jit(solution)/shard_map/all_to_all | solution.py:215
  18.7 7.1 %collective-permute-start = (f32[8,128]{1,0:T(8,128)S(1)}, f32[8,128]{1,0:T(8,128)S(1)}, u32[]{:S(2)}, u32[]{:S(2)}) collective-permute-start(f32[8,128]{1,0:T(8,128)S(1)} %reduce_sum.9.a_ref), channel_id=1, source_target_pairs={{0,36},{4,32},{8,44},{12,40},{16,52},{20,48},{24,60},{28,56},{32,4... | collective-permute-start | bytes 12296 | tf_op jit(solution)/shard_map/ppermute | solution.py:217
  25.8 1.3 %collective-permute-done.b_ref = f32[8,128]{1,0:T(8,128)S(1)} collective-permute-done((f32[8,128]{1,0:T(8,128)S(1)}, f32[8,128]{1,0:T(8,128)S(1)}, u32[]{:S(2)}, u32[]{:S(2)}) %collective-permute-start) | collective-permute-done | bytes 4128 | tf_op jit(solution)/shard_map/ppermute | solution.py:217
  27.1 0.4 cuts.1
  27.5 10.0 %all_to_all.11 = f32[32,4,128]{2,1,0:T(4,128)S(1)} all-to-all(f32[32,4,128]{2,1,0:T(4,128)S(1)} %cuts.1), channel_id=1, replica_groups={{144,148,152,156,128,132,136,140,208,212,216,220,192,196,200,204,16,20,..., dimensions={0} | all-to-all | bytes 131072 | tf_op jit(solution)/shard_map/all_to_all | solution.py:219
  37.5 0.6 %copy.5 = f32[128,128]{1,0:T(8,128)} copy(f32[128,128]{1,0:T(8,128)S(1)} %bitcast.3) | data formatting | bytes 131072
  (1 shorter events, 0.0 us)
Async XLA Ops:
  18.7 8.4 %collective-permute-start = (f32[8,128]{1,0:T(8,128)S(1)}, f32[8,128]{1,0:T(8,128)S(1)}, u32[]{:S(2)}, u32[]{:S(2)}) collective-permute-start(f32[8,128]{1,0:T(8,128)S(1)} %reduce_sum.9.a_ref), channel_id=1, source_target_pairs={{0,36},{4,32},{8,44},{12,40},{16,52},{20,48},{24,60},{28,56},{32,4... | collective-permute-start | bytes 12296 | tf_op jit(solution)/shard_map/ppermute | solution.py:217
